TPU v7x, 32 devices: a whole 2x2x4 slice. The times are simulated.
32 devices in a mesh: group: 2 (over y), seq: 16 (over z, x, core), tensor: 1.
Axes of the slice: x: 2, y: 2, z: 4, core: 2. Of those that a mesh axis runs over, the one named last changes fastest.
Arguments:
- queries: bfloat16 [64, 64, 128], P('group', 'tensor'), parts along dimension 0, may hold values from -10 to 10
- k_cache: bfloat16 [256, 8, 128, 128], P(('group', 'seq'), 'tensor'), parts along dimension 0, may hold values from -6 to 6
- value_cache: bfloat16 [256, 8, 128, 128], P(('group', 'seq'), 'tensor'), parts along dimension 0, may hold values from -6 to 6
- kv_lengths: int32 [64], P('group'), parts along dimension 0, may hold values from 1 to 4096, as said below
- page_table: int32 [64, 32], P('group'), parts along dimension 0, may hold values from -1 to 127, as said below
- request_batch_row: int32 [64], P('group'), parts along dimension 0, may hold values from 0 to 31, each once
Outputs:
- attended: bfloat16 [64, 64, 128], P('group', 'tensor'), parts along dimension 0
There are 2 independent parts, one for each index of `group`. A program takes and returns all parts, laid end to end along the dimension named above; each array names one. Nothing has to cross between parts.
Inputs may be any that keep to these rules, and one draw needn't show every extreme that they name: `kv_lengths`: the longest request holds exactly 4096 tokens. `page_table`: row r lists in order the cache slots of the first ceil(kv_lengths[r] / 128) pages of request r and -1 after them; no slot is listed twice.
All inputs are finite; a program needn't handle non-finite values.
Results may differ from a plain program's by a relative error of at most 0.0042.
Values may be sent and summed in bfloat16 or wider, within the bound.
A program may use at most 64 MiB of HBM per device.

v0:
```python
import jax
import jax.numpy as jnp
from jax import lax
from jax.sharding import PartitionSpec as P

NEG_BIG = -1e30


def slot_owners(page_table, first_slot, slot_count):
    global_ids = first_slot + jnp.arange(slot_count, dtype=jnp.int32)
    match_int = (page_table[None, :, :] == global_ids[:, None, None]).astype(jnp.int32)
    request_ids = jnp.arange(page_table.shape[0], dtype=jnp.int32)
    page_ids = jnp.arange(page_table.shape[1], dtype=jnp.int32)
    owner_ids = jnp.sum(match_int * request_ids[None, :, None], axis=(1, 2))
    logical = jnp.sum(match_int * page_ids[None, None, :], axis=(1, 2))
    live_mask = jnp.sum(match_int, axis=(1, 2)) > 0
    return (owner_ids, logical, live_mask)


def page_partials(q_rows, key_pages, value_pages, owner_ids, logical, live_mask, kv_lengths):
    slot_count, heads_kv, page_len, head_dim = key_pages.shape
    group_width = q_rows.shape[1] // heads_kv
    slot_queries = jnp.take(q_rows, owner_ids, axis=0).reshape(
        slot_count, heads_kv, group_width, head_dim
    )
    scores = jnp.einsum(
        "skgd,sktd->skgt", slot_queries, key_pages, preferred_element_type=jnp.float32
    ) * head_dim ** (-0.5)
    positions = logical[:, None] * page_len + jnp.arange(page_len, dtype=jnp.int32)[None, :]
    valid_mask = live_mask[:, None] & (positions < jnp.take(kv_lengths, owner_ids)[:, None])
    valid_wide = valid_mask[:, None, None, :]
    masked = jnp.where(valid_wide, scores, NEG_BIG)
    page_max = jnp.max(masked, axis=3)
    weights = jnp.where(valid_wide, jnp.exp(masked - page_max[..., None]), 0.0)
    page_sum = jnp.sum(weights, axis=3)
    page_out = jnp.einsum(
        "skgt,sktd->skgd",
        weights.astype(jnp.bfloat16),
        value_pages,
        preferred_element_type=jnp.float32,
    )
    return (
        page_max.reshape(slot_count, -1),
        page_sum.reshape(slot_count, -1),
        page_out.reshape(slot_count, -1),
    )


def request_partials(page_max, page_sum, page_out, owner_ids, live_mask, requests, head_dim):
    slot_count, heads_local = page_max.shape
    owned = (owner_ids[:, None] == jnp.arange(requests, dtype=jnp.int32)[None, :]) & live_mask[
        :, None
    ]
    req_max = jnp.max(jnp.where(owned[:, :, None], page_max[:, None, :], NEG_BIG), axis=0)
    factor = jnp.where(
        live_mask[:, None], jnp.exp(page_max - jnp.take(req_max, owner_ids, axis=0)), 0.0
    )
    owned_float = owned.astype(jnp.float32)
    req_sum = jnp.einsum(
        "sr,sh->rh", owned_float, page_sum * factor, precision=lax.Precision.HIGHEST
    )
    scaled = (page_out.reshape(slot_count, heads_local, head_dim) * factor[..., None]).reshape(
        slot_count, -1
    )
    req_out = jnp.einsum("sr,sx->rx", owned_float, scaled, precision=lax.Precision.HIGHEST)
    return (req_max, req_sum, req_out.reshape(requests, heads_local, head_dim))


def shards(queries, k_cache, value_cache, kv_lengths, page_table, request_batch_row):
    slot_count = k_cache.shape[0]
    requests = queries.shape[0]
    heads_local = queries.shape[1]
    head_dim = queries.shape[2]
    first_slot = lax.axis_index("seq") * slot_count
    owner_ids, logical, live_mask = slot_owners(page_table, first_slot, slot_count)
    q_rows = jnp.take(queries, request_batch_row, axis=0)
    page_max, page_sum, page_out = page_partials(
        q_rows, k_cache, value_cache, owner_ids, logical, live_mask, kv_lengths
    )
    owner_used, live_used = (owner_ids, live_mask)
    req_max, req_sum, req_out = request_partials(
        page_max, page_sum, page_out, owner_used, live_used, requests, head_dim
    )
    overall = lax.pmax(req_max, "seq")
    factor = jnp.exp(req_max - overall)
    flat_sum = (req_sum * factor).reshape(-1)
    flat_out = (req_out * factor[..., None]).reshape(requests * heads_local, head_dim)
    part_out, part_sum = (
        lax.psum_scatter(flat_out, "seq", scatter_dimension=0, tiled=True),
        lax.psum_scatter(flat_sum, "seq", scatter_dimension=0, tiled=True),
    )
    finished = (part_out / part_sum[:, None]).astype(jnp.bfloat16)
    result = lax.all_gather(finished, "seq", axis=0, tiled=True).reshape(
        requests, heads_local, head_dim
    )
    return jnp.zeros_like(queries).at[request_batch_row].set(result)


def solution(mesh):
    return jax.shard_map(
        shards,
        mesh=mesh,
        in_specs=(
            P("group", "tensor", None),
            P(("group", "seq"), "tensor", None, None),
            P(("group", "seq"), "tensor", None, None),
            P("group"),
            P("group", None),
            P("group"),
        ),
        out_specs=P("group", "tensor", None),
        check_vma=False,
    )
```

profile of v0, /device:TPU:1, one launch (start us, length us, event | category | flops | bytes accessed | tf_op | source)
XLA Modules:
  0.0 172.1 jit_solution(439582265242528450)
XLA Ops:
  6.5 0.8 compare_select_fusion.4
  7.3 0.7 compare_and_fusion
  8.0 1.3 fusion.8
  9.4 1.3 gather_fusion
  10.7 1.7 gather_fusion.1
  12.4 0.1 broadcast_select_fusion
  12.5 0.6 gather_fusion.2
  13.1 0.1 fusion.18
  13.2 0.1 fusion.19
  13.2 1.3 fusion.26
  14.5 0.1 reshape.182
  14.6 0.1 select_reduce_fusion
  14.7 0.6 gather_fusion.3
  15.3 57.9 %pmax.7 = f32[32,64]{1,0:T(8,128)S(1)} all-reduce(f32[32,64]{1,0:T(8,128)S(1)} %select_reduce_fusion), channel_id=1, replica_groups=mesh['group'=2,'seq'=16,'tensor'=1] {'seq'}, use_global_device_ids=true, to_apply=%region_5.6 | all-reduce | flops 2048 | bytes 16384 | tf_op jit(solution)/shard_map/pmax | solution.py:84
  73.2 0.1 exponential_select_fusion.1
  73.3 0.1 copy.15
  73.4 0.1 copy.16
  73.5 2.3 %convolution_bitcast_fusion = f32[1,8,64,128]{3,2,1,0:T(8,128)S(1)} fusion(bf16[8,8,128,128]{3,2,1,0:T(8,128)(2,1)} %param.8, f32[8,8,8,128]{3,2,1,0:T(8,128)S(1)} %get-tuple-element.11, f32[8,8,8]{2,1,0:T(8,128)S(1)} %get-tuple-element.10, pred[8,128]{1,0:T(8,128)(4,1)S(1)} %fusion.19), kind=kOutput, calls=%fused_computation.8 | convolution fusion | flops 16973824 | bytes 2624512 | tf_op jit(solution)/shard_map/skgt,sktd->skgd/dot_general | solution.py:36
  75.8 0.7 convolution_multiply_fusion
  76.5 1.6 copy.17
  78.2 0.3 fusion.5
  78.4 0.1 reshape.184
  78.5 0.3 convolution_multiply_fusion.2
  78.8 0.1 reshape.185
  78.9 0.6 dynamic-slice
  80.1 34.5 %all-reduce = f32[2048]{0:T(1024)S(1)} all-reduce(f32[2048]{0:T(1024)S(1)} %reshape.185), channel_id=3, replica_groups=mesh['group'=2,'seq'=16,'tensor'=1] {'seq'}, use_global_device_ids=true, to_apply=%region_8.9.clone | all-reduce | flops 2048 | bytes 16384
  114.6 0.1 dynamic-slice.1
  114.7 21.2 %reduce-scatter.2.cloned.1.call-done = f32[128,128]{1,0:T(8,128)} async-done(((f32[2048,128]{1,0:T(8,128)}), f32[128,128]{1,0:T(8,128)}) %reduce-scatter.2.cloned.1.call-update) | async-done | bytes 65552 | tf_op jit(solution)/shard_map/reduce_scatter | solution.py:89
  135.9 0.9 divide_convert_fusion
  136.8 23.1 %all_gather.3 = bf16[2048,128]{1,0:T(8,128)(2,1)S(1)} all-gather(bf16[128,128]{1,0:T(8,128)(2,1)S(1)} %divide_convert_fusion), channel_id=1, replica_groups=mesh['group'=2,'seq'=16,'tensor'=1] {'seq'}, dimensions={0}, use_global_device_ids=true | all-gather | bytes 557056 | tf_op jit(solution)/shard_map/all_gather | solution.py:93
  160.0 0.9 broadcast_in_dim.106
  160.9 4.4 %scatter_fusion = bf16[32,64,128]{2,1,0:T(8,128)(2,1)} fusion(bf16[32,64,128]{2,1,0:T(8,128)(2,1)} %broadcast_in_dim.106, s32[32]{0:T(128)S(1)} %compare_select_fusion.4, bf16[32,64,128]{2,1,0:T(8,128)(2,1)S(1)} %bitcast.36), kind=kCustom, calls=%fused_computation.4 | custom fusion | bytes 1572992 | tf_op jit(solution)/shard_map/scatter | solution.py:96
  (13 shorter events, 0.1 us)
Async XLA Ops:
  6.5 6.7 %copy-start = (bf16[8,8,128,128]{3,2,1,0:T(8,128)(2,1)S(1)}, bf16[8,8,128,128]{3,2,1,0:T(8,128)(2,1)}, u32[]{:S(2)}) copy-start(bf16[8,8,128,128]{3,2,1,0:T(8,128)(2,1)} %param.7) | copy-start | bytes 6291460
  6.5 129.4 %reduce-scatter.2.cloned.1.call-start = ((), (), s32[]{:S(2)}) async-start(), calls=%async_computation.1 | async-start | bytes 1114112 | tf_op jit(solution)/shard_map/reduce_scatter | solution.py:89
  76.5 2.4 %copy-start.1 = (u32[32]{0:T(128)S(1)}, u32[32]{0:T(128)}, u32[]{:S(2)}) copy-start(u32[32]{0:T(128)} %constant.82) | copy-start | bytes 388
Sparse Core Ops, SparseCore 0:
  78.3 57.5 reduce-scatter.1
where the time goes:
time: 173 us; the launch traced here: 172 us
  blocking collectives  116 us (67%)
  waiting for transfers between devices  21.2 us (12%)
  between operations  14.2 us (8%)
  local copies, waits for them, and re-layouts  12.1 us (7%)
  matrix products  4.56 us (3%)
  other arithmetic  4.46 us (3%)
    pmax x1, blocking collectives, shards(): overall = lax.pmax(req_max, 'seq')  57.9 us
    unnamed x1, blocking collectives  34.5 us
    all_gather x1, blocking collectives, shards(): lax.all_gather(finished, 'seq', axis=0, tiled=True)  23.1 us
    reduce_scatter x1, waiting for transfers between devices, shards(): lax.psum_scatter(flat_out, 'seq', scatter_dimension=0, tiled=True)  21.2 us
    scatter x1, local copies, waits for them, and re-layouts, shards(): return jnp.zeros_like(queries).at[request_batch_row].set(result)  4.35 us
  transfers between devices with their start and end apart: 1, of which 1 were waited for; matrix products, arithmetic and copies ran while one was open for 1% of the time, Pallas kernels for 0%

commit v1 on v0

--- a/solution.py
+++ b/solution.py
@@ -1,6 +1,10 @@
+import functools
+
 import jax
 import jax.numpy as jnp
 from jax import lax
+from jax.experimental import pallas as pl
+from jax.experimental.pallas import tpu as pltpu
 from jax.sharding import PartitionSpec as P
 
 NEG_BIG = -1e30
@@ -66,7 +70,7 @@
     return (req_max, req_sum, req_out.reshape(requests, heads_local, head_dim))
 
 
-def shards(queries, k_cache, value_cache, kv_lengths, page_table, request_batch_row):
+def plain_shards(queries, k_cache, value_cache, kv_lengths, page_table, request_batch_row):
     slot_count = k_cache.shape[0]
     requests = queries.shape[0]
     heads_local = queries.shape[1]
@@ -96,7 +100,250 @@
     return jnp.zeros_like(queries).at[request_batch_row].set(result)
 
 
+def attend_kernel(
+    n,
+    rows_smem,
+    lens_smem,
+    rows_ref,
+    table_ref,
+    q_ref,
+    k_hbm,
+    v_hbm,
+    out_ref,
+    k_buf,
+    v_buf,
+    part,
+    x_send,
+    x_recv,
+    l_send,
+    l_recv,
+    piece,
+    k_sem,
+    v_sem,
+    xs_sem,
+    xr_sem,
+    ls_sem,
+    lr_sem,
+    gs_sem,
+    gr_sem,
+    fs_sem,
+    fr_sem,
+    own_sem,
+):
+    me = lax.axis_index("seq")
+    slots, heads_kv, page_len, head_dim = k_hbm.shape
+    requests, heads, _ = q_ref.shape
+    width = heads // heads_kv
+    mine = heads // n
+    pages = table_ref.shape[1]
+    total_slots = n * slots
+
+    def remote(src, dst, send_sem, recv_sem, target):
+        return pltpu.make_async_remote_copy(
+            src_ref=src,
+            dst_ref=dst,
+            send_sem=send_sem,
+            recv_sem=recv_sem,
+            device_id={"seq": target},
+            device_id_type=pl.DeviceIdType.MESH,
+        )
+
+    k_copies = [pltpu.make_async_copy(k_hbm.at[s], k_buf.at[s], k_sem.at[s]) for s in range(slots)]
+    v_copies = [pltpu.make_async_copy(v_hbm.at[s], v_buf.at[s], v_sem.at[s]) for s in range(slots)]
+    for s in range(slots):
+        k_copies[s].start()
+        v_copies[s].start()
+
+    barrier = pltpu.get_barrier_semaphore()
+    for o in range(1, n):
+        pl.semaphore_signal(
+            barrier,
+            inc=1,
+            device_id={"seq": lax.rem(me + o, n)},
+            device_id_type=pl.DeviceIdType.MESH,
+        )
+
+    table = table_ref[...]
+    code = lax.broadcasted_iota(jnp.int32, table.shape, 0) * pages + lax.broadcasted_iota(
+        jnp.int32, table.shape, 1
+    )
+    found = []
+    for s in range(slots):
+        found.append(jnp.max(jnp.where(table == me * slots + s, code, -1)))
+
+    lane = lax.broadcasted_iota(jnp.int32, (1, total_slots), 1)
+    token = lax.broadcasted_iota(jnp.int32, (1, page_len), 1)
+    lse = jnp.zeros((heads, total_slots), jnp.float32)
+    for s in range(slots):
+        at = jnp.maximum(found[s], 0)
+        request = at // pages
+        page = at - request * pages
+        left = jnp.where(found[s] >= 0, lens_smem[request] - page * page_len, 0)
+        q_rows = q_ref[rows_smem[request]]
+        k_copies[s].wait()
+        scores = jnp.concatenate(
+            [
+                lax.dot_general(
+                    q_rows[g * width : (g + 1) * width],
+                    k_buf[s, g],
+                    (((1,), (1,)), ((), ())),
+                    preferred_element_type=jnp.float32,
+                )
+                for g in range(heads_kv)
+            ],
+            axis=0,
+        ) * head_dim ** (-0.5)
+        masked = jnp.where(token < left, scores, NEG_BIG)
+        top = jnp.max(masked, axis=1, keepdims=True)
+        weights = jnp.exp(masked - top)
+        weight_sum = jnp.sum(weights, axis=1, keepdims=True)
+        lse = jnp.where(lane == me * slots + s, top + jnp.log(weight_sum), lse)
+        weights_bf = weights.astype(jnp.bfloat16)
+        inverse = 1.0 / weight_sum
+        v_copies[s].wait()
+        for g in range(heads_kv):
+            band = slice(g * width, (g + 1) * width)
+            out = jnp.dot(weights_bf[band], v_buf[s, g], preferred_element_type=jnp.float32)
+            part[band, s, :] = out * inverse[band]
+
+    l_send[...] = lse.reshape(n, mine, total_slots)
+    for j in range(n):
+        x_send[j] = part[j * mine : (j + 1) * mine].astype(jnp.bfloat16)
+
+    pl.semaphore_wait(barrier, n - 1)
+    first = []
+    for o in range(1, n):
+        to = lax.rem(me + o, n)
+        first.append(remote(l_send.at[to], l_recv.at[me], ls_sem.at[o], lr_sem.at[me], to))
+        first.append(remote(x_send.at[to], x_recv.at[me], xs_sem.at[o], xr_sem.at[me], to))
+    for copy in first:
+        copy.start()
+
+    x_recv[me] = x_send[me]
+    l_recv[me] = l_send[me]
+    owned = jnp.zeros((requests, total_slots), jnp.bool_)
+    for p in range(pages):
+        owned = owned | (table[:, p : p + 1] == lane)
+    place = (
+        lax.broadcasted_iota(jnp.int32, (requests, requests), 0) == rows_ref[...]
+    ).astype(jnp.float32).astype(jnp.bfloat16)
+    owned = (
+        jnp.dot(
+            place,
+            owned.astype(jnp.float32).astype(jnp.bfloat16),
+            preferred_element_type=jnp.float32,
+        )
+        > 0.5
+    )
+
+    for o in range(1, n):
+        source = lax.rem(me + o, n)
+        remote(l_send.at[0], l_recv.at[source], ls_sem.at[0], lr_sem.at[source], source).wait_recv()
+    lse_all = l_recv[0]
+    for j in range(1, n):
+        lse_all = lse_all + l_recv[j]
+    mixes = []
+    for h in range(mine):
+        level = jnp.where(owned, lse_all[h : h + 1], NEG_BIG)
+        peak = jnp.max(level, axis=1, keepdims=True)
+        mix = jnp.where(owned, jnp.exp(level - peak), 0.0)
+        mix = mix * (1.0 / jnp.sum(mix, axis=1, keepdims=True))
+        high = mix.astype(jnp.bfloat16)
+        low = (mix - high.astype(jnp.float32)).astype(jnp.bfloat16)
+        mixes.append((high, low))
+    for o in range(1, n):
+        source = lax.rem(me + o, n)
+        remote(x_send.at[0], x_recv.at[source], xs_sem.at[0], xr_sem.at[source], source).wait_recv()
+    for h in range(mine):
+        rows = jnp.concatenate([x_recv[j, h].astype(jnp.float32) for j in range(n)], axis=0).astype(
+            jnp.bfloat16
+        )
+        high, low = mixes[h]
+        done = jnp.dot(high, rows, preferred_element_type=jnp.float32) + jnp.dot(
+            low, rows, preferred_element_type=jnp.float32
+        )
+        piece[h] = done.astype(jnp.bfloat16)
+
+    partner = me + 1 - 2 * lax.rem(me, 2)
+    second = []
+    for o in range(2, n, 2):
+        to = lax.rem(me + o, n)
+        second.append(remote(piece, out_ref.at[me], gs_sem.at[o], gr_sem.at[me], to))
+    second.append(remote(piece, out_ref.at[me], fs_sem.at[0], fr_sem.at[me], partner))
+    for copy in second:
+        copy.start()
+    own = pltpu.make_async_copy(piece, out_ref.at[me], own_sem)
+    own.start()
+    passed = []
+    for o in range(2, n, 2):
+        source = lax.rem(me + o, n)
+        remote(piece, out_ref.at[source], gs_sem.at[0], gr_sem.at[source], source).wait_recv()
+        on = remote(
+            out_ref.at[source], out_ref.at[source], fs_sem.at[o], fr_sem.at[source], partner
+        )
+        on.start()
+        passed.append(on)
+    for o in range(0, n, 2):
+        source = lax.rem(partner + o, n)
+        remote(piece, out_ref.at[source], fs_sem.at[0], fr_sem.at[source], partner).wait_recv()
+    own.wait()
+    for copy in first + second + passed:
+        copy.wait_send()
+
+
+def seq_shards(n, queries, k_cache, value_cache, kv_lengths, page_table, request_batch_row):
+    slots, heads_kv, page_len, head_dim = k_cache.shape
+    requests, heads, _ = queries.shape
+    if heads % n or n % 2:
+        return plain_shards(
+            queries, k_cache, value_cache, kv_lengths, page_table, request_batch_row
+        )
+    mine = heads // n
+    smem = pl.BlockSpec(memory_space=pltpu.SMEM)
+    vmem = pl.BlockSpec(memory_space=pltpu.VMEM)
+    anywhere = pl.BlockSpec(memory_space=pl.ANY)
+    sems = pltpu.SemaphoreType.DMA
+    out = pl.pallas_call(
+        functools.partial(attend_kernel, n),
+        out_shape=jax.ShapeDtypeStruct((n, mine, requests, head_dim), queries.dtype),
+        in_specs=[smem, smem, vmem, vmem, vmem, anywhere, anywhere],
+        out_specs=vmem,
+        scratch_shapes=[
+            pltpu.VMEM(k_cache.shape, k_cache.dtype),
+            pltpu.VMEM(value_cache.shape, value_cache.dtype),
+            pltpu.VMEM((heads, slots, head_dim), jnp.float32),
+            pltpu.VMEM((n, mine, slots, head_dim), jnp.bfloat16),
+            pltpu.VMEM((n, mine, slots, head_dim), jnp.bfloat16),
+            pltpu.VMEM((n, mine, n * slots), jnp.float32),
+            pltpu.VMEM((n, mine, n * slots), jnp.float32),
+            pltpu.VMEM((mine, requests, head_dim), jnp.bfloat16),
+            sems((slots,)),
+            sems((slots,)),
+            sems((n,)),
+            sems((n,)),
+            sems((n,)),
+            sems((n,)),
+            sems((n,)),
+            sems((n,)),
+            sems((n,)),
+            sems((n,)),
+            sems,
+        ],
+        compiler_params=pltpu.CompilerParams(collective_id=0, has_side_effects=True),
+    )(
+        request_batch_row,
+        kv_lengths,
+        request_batch_row.reshape(1, requests),
+        page_table,
+        queries,
+        k_cache,
+        value_cache,
+    )
+    return out.reshape(heads, requests, head_dim).transpose(1, 0, 2)
+
+
 def solution(mesh):
+    shards = functools.partial(seq_shards, mesh.shape["seq"])
     return jax.shard_map(
         shards,
         mesh=mesh,

time: 173 us -> 27.4 us (0.16)
  blocking collectives: 116 us -> 0 us
  Pallas kernels: 0 us -> 25.1 us
  waiting for transfers between devices: 21.2 us -> 0 us
  between operations: 14.2 us -> 0.01 us
  local copies, waits for them, and re-layouts: 12.1 us -> 2.04 us
  matrix products: 4.56 us -> 0 us
  other arithmetic: 4.46 us -> 0 us
    pmax x1 -> x0, blocking collectives: 57.9 us -> none  [shards(): overall = lax.pmax(req_max, 'seq')]
    unnamed x1 -> x0, blocking collectives: 34.5 us -> none
    pallas_call x0 -> x1, Pallas kernels: none -> 25.1 us  [seq_shards(): pl.pallas_call(functools.partial(attend_kernel, n), out_shape=jax.ShapeDt...]
    all_gather x1 -> x0, blocking collectives: 23.1 us -> none  [shards(): lax.all_gather(finished, 'seq', axis=0, tiled=True)]
    reduce_scatter x1 -> x0, waiting for transfers between devices: 21.2 us -> none  [shards(): lax.psum_scatter(flat_out, 'seq', scatter_dimension=0, tiled=True)]
    dot_general x4 -> x0, matrix products: 4.56 us -> none  [the longest x1 2.29 us: page_partials(): jnp.einsum('skgt,sktd->skgd', weights.astype(jnp.bfloat16), value_pages,...]
    scatter x1 -> x0, local copies, waits for them, and re-layouts: 4.35 us -> none  [shards(): return jnp.zeros_like(queries).at[request_batch_row].set(result)]
    gather x4 -> x0, local copies, waits for them, and re-layouts: 4.12 us -> none  [the longest x1 1.69 us: shards(): q_rows = jnp.take(queries, request_batch_row, axis=0)]
  transfers between devices with their start and end apart: 1 -> 0, of which waited for: 1 -> 0; matrix products, arithmetic and copies ran while one was open for 1% -> 0% of each run, Pallas kernels for 0% -> 0%
where the time goes in v1:
time: 27.4 us; the launch traced here: 27.1 us
  Pallas kernels  25.1 us (92%)
  local copies, waits for them, and re-layouts  2.04 us (7%)
    pallas_call x1, Pallas kernels, seq_shards(): pl.pallas_call(functools.partial(attend_kernel, n), out_shape=jax.ShapeDt...  25.1 us
    reshape x1, local copies, waits for them, and re-layouts, seq_shards(): return out.reshape(heads, requests, head_dim).transpose(1, 0, 2)  2.04 us

profile of v1, /device:TPU:1, one launch (start us, length us, event | category | flops | bytes accessed | tf_op | source)
XLA Modules:
  0.0 27.1 jit_solution(9319092312124738930)
XLA Ops:
  0.0 25.1 %shard_map.64 = bf16[16,4,32,128]{3,2,1,0:T(8,128)(2,1)} custom-call(s32[32]{0:T(128)} %rows_smem.1, s32[32]{0:T(128)} %lens_smem.1, s32[1,32]{1,0:T(1,128)} %bitcast.6, s32[32,32]{1,0:T(8,128)} %table_ref.1, bf16[32,64,128]{2,1,0:T(8,128)(2,1)} %q_ref.1, bf16[8,8,128,128]{3,2,1,0:T(8,128)(2,1)} %k_hbm.1, bf16[8,8,128,128]{3,2,1,0:T(8,128)(2,1)} %v_hbm.1), custom_call_target="tpu_custom_call" | custom-call | tf_op jit(solution)/shard_map/pallas_call | solution.py:306
  25.1 2.0 %copy.9 = bf16[64,32,128]{2,0,1:T(8,128)(2,1)} copy(bf16[64,32,128]{2,1,0:T(8,128)(2,1)} %bitcast.5) | data formatting | bytes 1048576 | tf_op jit(solution)/shard_map/reshape | solution.py:342

commit v2 on v1

--- a/solution.py
+++ b/solution.py
@@ -106,10 +106,11 @@
     lens_smem,
     rows_ref,
     table_ref,
-    q_ref,
+    q_hbm,
     k_hbm,
     v_hbm,
     out_ref,
+    q_ref,
     k_buf,
     v_buf,
     part,
@@ -118,6 +119,9 @@
     l_send,
     l_recv,
     piece,
+    pieces,
+    wide,
+    q_sem,
     k_sem,
     v_sem,
     xs_sem,
@@ -128,7 +132,6 @@
     gr_sem,
     fs_sem,
     fr_sem,
-    own_sem,
 ):
     me = lax.axis_index("seq")
     slots, heads_kv, page_len, head_dim = k_hbm.shape
@@ -148,21 +151,24 @@
             device_id_type=pl.DeviceIdType.MESH,
         )
 
+    far_first = sorted(range(1, n), key=lambda o: abs(o - n // 2))
+    q_copy = pltpu.make_async_copy(q_hbm, q_ref, q_sem)
+    q_copy.start()
+    barrier = pltpu.get_barrier_semaphore()
+    for o in far_first:
+        pl.semaphore_signal(
+            barrier,
+            inc=1,
+            device_id={"seq": lax.rem(me + o, n)},
+            device_id_type=pl.DeviceIdType.MESH,
+        )
+
     k_copies = [pltpu.make_async_copy(k_hbm.at[s], k_buf.at[s], k_sem.at[s]) for s in range(slots)]
     v_copies = [pltpu.make_async_copy(v_hbm.at[s], v_buf.at[s], v_sem.at[s]) for s in range(slots)]
     for s in range(slots):
         k_copies[s].start()
         v_copies[s].start()
 
-    barrier = pltpu.get_barrier_semaphore()
-    for o in range(1, n):
-        pl.semaphore_signal(
-            barrier,
-            inc=1,
-            device_id={"seq": lax.rem(me + o, n)},
-            device_id_type=pl.DeviceIdType.MESH,
-        )
-
     table = table_ref[...]
     code = lax.broadcasted_iota(jnp.int32, table.shape, 0) * pages + lax.broadcasted_iota(
         jnp.int32, table.shape, 1
@@ -173,6 +179,7 @@
 
     lane = lax.broadcasted_iota(jnp.int32, (1, total_slots), 1)
     token = lax.broadcasted_iota(jnp.int32, (1, page_len), 1)
+    q_copy.wait()
     lse = jnp.zeros((heads, total_slots), jnp.float32)
     for s in range(slots):
         at = jnp.maximum(found[s], 0)
@@ -212,7 +219,7 @@
 
     pl.semaphore_wait(barrier, n - 1)
     first = []
-    for o in range(1, n):
+    for o in far_first:
         to = lax.rem(me + o, n)
         first.append(remote(l_send.at[to], l_recv.at[me], ls_sem.at[o], lr_sem.at[me], to))
         first.append(remote(x_send.at[to], x_recv.at[me], xs_sem.at[o], xr_sem.at[me], to))
@@ -265,28 +272,34 @@
         piece[h] = done.astype(jnp.bfloat16)
 
     partner = me + 1 - 2 * lax.rem(me, 2)
+    far_even = [o for o in far_first if o % 2 == 0]
+    near_even = far_even[::-1]
     second = []
-    for o in range(2, n, 2):
+    for o in far_even:
         to = lax.rem(me + o, n)
-        second.append(remote(piece, out_ref.at[me], gs_sem.at[o], gr_sem.at[me], to))
-    second.append(remote(piece, out_ref.at[me], fs_sem.at[0], fr_sem.at[me], partner))
+        second.append(remote(piece, pieces.at[me], gs_sem.at[o], gr_sem.at[me], to))
+    second.append(remote(piece, pieces.at[me], fs_sem.at[0], fr_sem.at[me], partner))
     for copy in second:
         copy.start()
-    own = pltpu.make_async_copy(piece, out_ref.at[me], own_sem)
-    own.start()
+
+    def spread(block, source):
+        for h in range(mine):
+            wide[:, source * mine + h, :] = block[h].astype(jnp.float32)
+
+    spread(piece, me)
     passed = []
-    for o in range(2, n, 2):
+    for o in near_even:
         source = lax.rem(me + o, n)
-        remote(piece, out_ref.at[source], gs_sem.at[0], gr_sem.at[source], source).wait_recv()
-        on = remote(
-            out_ref.at[source], out_ref.at[source], fs_sem.at[o], fr_sem.at[source], partner
-        )
+        remote(piece, pieces.at[source], gs_sem.at[0], gr_sem.at[source], source).wait_recv()
+        on = remote(pieces.at[source], pieces.at[source], fs_sem.at[o], fr_sem.at[source], partner)
         on.start()
         passed.append(on)
-    for o in range(0, n, 2):
+        spread(pieces.at[source], source)
+    for o in [0] + near_even:
         source = lax.rem(partner + o, n)
-        remote(piece, out_ref.at[source], fs_sem.at[0], fr_sem.at[source], partner).wait_recv()
-    own.wait()
+        remote(piece, pieces.at[source], fs_sem.at[0], fr_sem.at[source], partner).wait_recv()
+        spread(pieces.at[source], source)
+    out_ref[...] = wide[...].astype(out_ref.dtype)
     for copy in first + second + passed:
         copy.wait_send()
 
@@ -305,10 +318,11 @@
     sems = pltpu.SemaphoreType.DMA
     out = pl.pallas_call(
         functools.partial(attend_kernel, n),
-        out_shape=jax.ShapeDtypeStruct((n, mine, requests, head_dim), queries.dtype),
-        in_specs=[smem, smem, vmem, vmem, vmem, anywhere, anywhere],
+        out_shape=pltpu.VMEM(queries.shape, queries.dtype),
+        in_specs=[smem, smem, vmem, vmem, anywhere, anywhere, anywhere],
         out_specs=vmem,
         scratch_shapes=[
+            pltpu.VMEM(queries.shape, queries.dtype),
             pltpu.VMEM(k_cache.shape, k_cache.dtype),
             pltpu.VMEM(value_cache.shape, value_cache.dtype),
             pltpu.VMEM((heads, slots, head_dim), jnp.float32),
@@ -317,6 +331,9 @@
             pltpu.VMEM((n, mine, n * slots), jnp.float32),
             pltpu.VMEM((n, mine, n * slots), jnp.float32),
             pltpu.VMEM((mine, requests, head_dim), jnp.bfloat16),
+            pltpu.VMEM((n, mine, requests, head_dim), jnp.bfloat16),
+            pltpu.VMEM(queries.shape, jnp.float32),
+            sems,
             sems((slots,)),
             sems((slots,)),
             sems((n,)),
@@ -327,7 +344,6 @@
             sems((n,)),
             sems((n,)),
             sems((n,)),
-            sems,
         ],
         compiler_params=pltpu.CompilerParams(collective_id=0, has_side_effects=True),
     )(
@@ -339,7 +355,7 @@
         k_cache,
         value_cache,
     )
-    return out.reshape(heads, requests, head_dim).transpose(1, 0, 2)
+    return out
 
 
 def solution(mesh):

time: 27.4 us -> 25.6 us (0.934)
  local copies, waits for them, and re-layouts: 2.04 us -> 0.8 us
  Pallas kernels: 25.1 us -> 24.5 us
    reshape x1 -> x0, local copies, waits for them, and re-layouts: 2.04 us -> none  [seq_shards(): return out.reshape(heads, requests, head_dim).transpose(1, 0, 2)]
    unnamed x0 -> x1, local copies, waits for them, and re-layouts: none -> 0.8 us
    pallas_call x1, Pallas kernels: 25.1 us -> 24.5 us  [seq_shards(): pl.pallas_call(functools.partial(attend_kernel, n), out_shape=pltpu.VMEM(...]
where the time goes in v2:
time: 25.6 us; the launch traced here: 25.4 us
  Pallas kernels  24.5 us (96%)
  local copies, waits for them, and re-layouts  0.8 us (3%)
    pallas_call x1, Pallas kernels, seq_shards(): pl.pallas_call(functools.partial(attend_kernel, n), out_shape=pltpu.VMEM(...  24.5 us
    unnamed x1, local copies, waits for them, and re-layouts  0.8 us

profile of v2, /device:TPU:1, one launch (start us, length us, event | category | flops | bytes accessed | tf_op | source)
XLA Modules:
  0.0 25.4 jit_solution(16297883608902237704)
XLA Ops:
  0.0 24.5 %shard_map.64 = bf16[32,64,128]{2,1,0:T(8,128)(2,1)S(1)} custom-call(s32[32]{0:T(128)} %rows_smem.1, s32[32]{0:T(128)} %lens_smem.1, s32[1,32]{1,0:T(1,128)} %bitcast.1, s32[32,32]{1,0:T(8,128)} %table_ref.1, bf16[32,64,128]{2,1,0:T(8,128)(2,1)} %q_hbm.1, bf16[8,8,128,128]{3,2,1,0:T(8,128)(2,1)} %k_hbm.1, bf16[8,8,128,128]{3,2,1,0:T(8,128)(2,1)} %v_hbm.1), custom_call_target="tpu_custom_call" | custom-call | tf_op jit(solution)/shard_map/pallas_call | solution.py:319
  24.6 0.8 %copy.8 = bf16[32,64,128]{2,1,0:T(8,128)(2,1)} copy(bf16[32,64,128]{2,1,0:T(8,128)(2,1)S(1)} %shard_map.64) | data formatting | bytes 1048576

commit v3 on v2

--- a/solution.py
+++ b/solution.py
@@ -98,6 +98,9 @@
         requests, heads_local, head_dim
     )
     return jnp.zeros_like(queries).at[request_batch_row].set(result)
+
+
+BATCHES = 1
 
 
 def attend_kernel(
@@ -163,11 +166,20 @@
             device_id_type=pl.DeviceIdType.MESH,
         )
 
-    k_copies = [pltpu.make_async_copy(k_hbm.at[s], k_buf.at[s], k_sem.at[s]) for s in range(slots)]
-    v_copies = [pltpu.make_async_copy(v_hbm.at[s], v_buf.at[s], v_sem.at[s]) for s in range(slots)]
-    for s in range(slots):
-        k_copies[s].start()
-        v_copies[s].start()
+    batch = slots // BATCHES if slots % BATCHES == 0 else slots
+    batches = [range(at, at + batch) for at in range(0, slots, batch)]
+
+    def fetch(source, buffer, sem):
+        copies = []
+        for i in range(len(batches)):
+            some = pl.ds(i * batch, batch)
+            copies.append(pltpu.make_async_copy(source.at[some], buffer.at[some], sem.at[i]))
+        return copies
+
+    k_copies = fetch(k_hbm, k_buf, k_sem)
+    v_copies = fetch(v_hbm, v_buf, v_sem)
+    for copy in k_copies + v_copies:
+        copy.start()
 
     table = table_ref[...]
     code = lax.broadcasted_iota(jnp.int32, table.shape, 0) * pages + lax.broadcasted_iota(
@@ -181,37 +193,41 @@
     token = lax.broadcasted_iota(jnp.int32, (1, page_len), 1)
     q_copy.wait()
     lse = jnp.zeros((heads, total_slots), jnp.float32)
-    for s in range(slots):
-        at = jnp.maximum(found[s], 0)
-        request = at // pages
-        page = at - request * pages
-        left = jnp.where(found[s] >= 0, lens_smem[request] - page * page_len, 0)
-        q_rows = q_ref[rows_smem[request]]
-        k_copies[s].wait()
-        scores = jnp.concatenate(
-            [
-                lax.dot_general(
-                    q_rows[g * width : (g + 1) * width],
-                    k_buf[s, g],
-                    (((1,), (1,)), ((), ())),
-                    preferred_element_type=jnp.float32,
-                )
-                for g in range(heads_kv)
-            ],
-            axis=0,
-        ) * head_dim ** (-0.5)
-        masked = jnp.where(token < left, scores, NEG_BIG)
-        top = jnp.max(masked, axis=1, keepdims=True)
-        weights = jnp.exp(masked - top)
-        weight_sum = jnp.sum(weights, axis=1, keepdims=True)
-        lse = jnp.where(lane == me * slots + s, top + jnp.log(weight_sum), lse)
-        weights_bf = weights.astype(jnp.bfloat16)
-        inverse = 1.0 / weight_sum
-        v_copies[s].wait()
-        for g in range(heads_kv):
-            band = slice(g * width, (g + 1) * width)
-            out = jnp.dot(weights_bf[band], v_buf[s, g], preferred_element_type=jnp.float32)
-            part[band, s, :] = out * inverse[band]
+    kept = []
+    for i, some in enumerate(batches):
+        k_copies[i].wait()
+        for s in some:
+            at = jnp.maximum(found[s], 0)
+            request = at // pages
+            page = at - request * pages
+            left = jnp.where(found[s] >= 0, lens_smem[request] - page * page_len, 0)
+            row = rows_smem[request]
+            scores = jnp.concatenate(
+                [
+                    lax.dot_general(
+                        q_ref[row, g * width : (g + 1) * width, :],
+                        k_buf[s, g],
+                        (((1,), (1,)), ((), ())),
+                        preferred_element_type=jnp.float32,
+                    )
+                    for g in range(heads_kv)
+                ],
+                axis=0,
+            ) * head_dim ** (-0.5)
+            masked = jnp.where(token < left, scores, NEG_BIG)
+            top = jnp.max(masked, axis=1, keepdims=True)
+            weights = jnp.exp(masked - top)
+            weight_sum = jnp.sum(weights, axis=1, keepdims=True)
+            lse = jnp.where(lane == me * slots + s, top + jnp.log(weight_sum), lse)
+            kept.append((weights.astype(jnp.bfloat16), 1.0 / weight_sum))
+    for i, some in enumerate(batches):
+        v_copies[i].wait()
+        for s in some:
+            weights_bf, inverse = kept[s]
+            for g in range(heads_kv):
+                band = slice(g * width, (g + 1) * width)
+                out = jnp.dot(weights_bf[band], v_buf[s, g], preferred_element_type=jnp.float32)
+                part[band, s, :] = out * inverse[band]
 
     l_send[...] = lse.reshape(n, mine, total_slots)
     for j in range(n):

time: 25.6 us -> 24.3 us (0.949)
  Pallas kernels: 24.5 us -> 23.3 us
    pallas_call x1, Pallas kernels: 24.5 us -> 23.3 us  [seq_shards(): pl.pallas_call(functools.partial(attend_kernel, n), out_shape=pltpu.VMEM(...]
where the time goes in v3:
time: 24.3 us; the launch traced here: 24.1 us
  Pallas kernels  23.3 us (96%)
  local copies, waits for them, and re-layouts  0.8 us (3%)
    pallas_call x1, Pallas kernels, seq_shards(): pl.pallas_call(functools.partial(attend_kernel, n), out_shape=pltpu.VMEM(...  23.3 us
    unnamed x1, local copies, waits for them, and re-layouts  0.8 us

profile of v3, /device:TPU:1, one launch (start us, length us, event | category | flops | bytes accessed | tf_op | source)
XLA Modules:
  0.0 24.1 jit_solution(2928015647745607181)
XLA Ops:
  0.0 23.3 %shard_map.64 = bf16[32,64,128]{2,1,0:T(8,128)(2,1)S(1)} custom-call(s32[32]{0:T(128)} %rows_smem.1, s32[32]{0:T(128)} %lens_smem.1, s32[1,32]{1,0:T(1,128)} %bitcast.1, s32[32,32]{1,0:T(8,128)} %table_ref.1, bf16[32,64,128]{2,1,0:T(8,128)(2,1)} %q_hbm.1, bf16[8,8,128,128]{3,2,1,0:T(8,128)(2,1)} %k_hbm.1, bf16[8,8,128,128]{3,2,1,0:T(8,128)(2,1)} %v_hbm.1), custom_call_target="tpu_custom_call" | custom-call | tf_op jit(solution)/shard_map/pallas_call | solution.py:335
  23.3 0.8 %copy.8 = bf16[32,64,128]{2,1,0:T(8,128)(2,1)} copy(bf16[32,64,128]{2,1,0:T(8,128)(2,1)S(1)} %shard_map.64) | data formatting | bytes 1048576

commit v4 on v3

--- a/solution.py
+++ b/solution.py
@@ -105,14 +105,18 @@
 
 def attend_kernel(
     n,
+    rows_hbm,
+    lens_hbm,
+    line_hbm,
+    table_hbm,
+    q_hbm,
+    k_hbm,
+    v_hbm,
+    out_ref,
     rows_smem,
     lens_smem,
     rows_ref,
     table_ref,
-    q_hbm,
-    k_hbm,
-    v_hbm,
-    out_ref,
     q_ref,
     k_buf,
     v_buf,
@@ -124,6 +128,7 @@
     piece,
     pieces,
     wide,
+    small_sem,
     q_sem,
     k_sem,
     v_sem,
@@ -154,9 +159,14 @@
             device_id_type=pl.DeviceIdType.MESH,
         )
 
+    small = [
+        pltpu.make_async_copy(table_hbm, table_ref, small_sem.at[0]),
+        pltpu.make_async_copy(rows_hbm, rows_smem, small_sem.at[1]),
+        pltpu.make_async_copy(lens_hbm, lens_smem, small_sem.at[2]),
+        pltpu.make_async_copy(line_hbm, rows_ref, small_sem.at[3]),
+    ]
     far_first = sorted(range(1, n), key=lambda o: abs(o - n // 2))
     q_copy = pltpu.make_async_copy(q_hbm, q_ref, q_sem)
-    q_copy.start()
     barrier = pltpu.get_barrier_semaphore()
     for o in far_first:
         pl.semaphore_signal(
@@ -178,8 +188,10 @@
 
     k_copies = fetch(k_hbm, k_buf, k_sem)
     v_copies = fetch(v_hbm, v_buf, v_sem)
-    for copy in k_copies + v_copies:
+    for copy in small + [q_copy] + k_copies + v_copies:
         copy.start()
+    for copy in small:
+        copy.wait()
 
     table = table_ref[...]
     code = lax.broadcasted_iota(jnp.int32, table.shape, 0) * pages + lax.broadcasted_iota(
@@ -328,16 +340,19 @@
             queries, k_cache, value_cache, kv_lengths, page_table, request_batch_row
         )
     mine = heads // n
-    smem = pl.BlockSpec(memory_space=pltpu.SMEM)
     vmem = pl.BlockSpec(memory_space=pltpu.VMEM)
     anywhere = pl.BlockSpec(memory_space=pl.ANY)
     sems = pltpu.SemaphoreType.DMA
     out = pl.pallas_call(
         functools.partial(attend_kernel, n),
         out_shape=pltpu.VMEM(queries.shape, queries.dtype),
-        in_specs=[smem, smem, vmem, vmem, anywhere, anywhere, anywhere],
+        in_specs=[anywhere] * 7,
         out_specs=vmem,
         scratch_shapes=[
+            pltpu.SMEM(request_batch_row.shape, jnp.int32),
+            pltpu.SMEM(kv_lengths.shape, jnp.int32),
+            pltpu.VMEM((1, requests), jnp.int32),
+            pltpu.VMEM(page_table.shape, jnp.int32),
             pltpu.VMEM(queries.shape, queries.dtype),
             pltpu.VMEM(k_cache.shape, k_cache.dtype),
             pltpu.VMEM(value_cache.shape, value_cache.dtype),
@@ -349,6 +364,7 @@
             pltpu.VMEM((mine, requests, head_dim), jnp.bfloat16),
             pltpu.VMEM((n, mine, requests, head_dim), jnp.bfloat16),
             pltpu.VMEM(queries.shape, jnp.float32),
+            sems((4,)),
             sems,
             sems((slots,)),
             sems((slots,)),

time: 24.3 us -> 23.5 us (0.967)
  Pallas kernels: 23.3 us -> 22.5 us
    pallas_call x1, Pallas kernels: 23.3 us -> 22.5 us  [seq_shards(): pl.pallas_call(functools.partial(attend_kernel, n), out_shape=pltpu.VMEM(...]
where the time goes in v4:
time: 23.5 us; the launch traced here: 23.3 us
  Pallas kernels  22.5 us (96%)
  local copies, waits for them, and re-layouts  0.8 us (3%)
    pallas_call x1, Pallas kernels, seq_shards(): pl.pallas_call(functools.partial(attend_kernel, n), out_shape=pltpu.VMEM(...  22.5 us
    unnamed x1, local copies, waits for them, and re-layouts  0.8 us

profile of v4, /device:TPU:1, one launch (start us, length us, event | category | flops | bytes accessed | tf_op | source)
XLA Modules:
  0.0 23.3 jit_solution(1778898563123887482)
XLA Ops:
  0.0 22.5 %shard_map.64 = bf16[32,64,128]{2,1,0:T(8,128)(2,1)S(1)} custom-call(s32[32]{0:T(128)} %rows_hbm.1, s32[32]{0:T(128)} %lens_hbm.1, s32[1,32]{1,0:T(1,128)} %bitcast.1, s32[32,32]{1,0:T(8,128)} %table_hbm.1, bf16[32,64,128]{2,1,0:T(8,128)(2,1)} %q_hbm.1, bf16[8,8,128,128]{3,2,1,0:T(8,128)(2,1)} %k_hbm.1, bf16[8,8,128,128]{3,2,1,0:T(8,128)(2,1)} %v_hbm.1), custom_call_target="tpu_custom_call" | custom-call | tf_op jit(solution)/shard_map/pallas_call | solution.py:346
  22.5 0.8 %copy.8 = bf16[32,64,128]{2,1,0:T(8,128)(2,1)} copy(bf16[32,64,128]{2,1,0:T(8,128)(2,1)S(1)} %shard_map.64) | data formatting | bytes 1048576
